TPU v7x, 128 devices: a whole 4x4x4 slice. The times are simulated.
128 devices in a mesh: dp: 8 (over x, core), mp: 16 (over y, z).
Axes of the slice: x: 4, y: 4, z: 4, core: 2. Of those that a mesh axis runs over, the one named last changes fastest.
Arguments:
- tokens: bfloat16 [256, 8192], P('dp', 'mp'), may hold values from -6 to 6
- gate_up_weight: bfloat16 [2, 8192, 15360], P(None, 'mp', 'dp'), may hold values from -0.0625 to 0.0625
- down_weight: bfloat16 [15360, 8192], P('dp', 'mp'), may hold values from -0.046875 to 0.046875
- gate_up_input_factor: bfloat16 [2, 8192, 64], P(None, 'mp'), may hold values from -0.0625 to 0.0625
- gate_up_output_factor: bfloat16 [2, 64, 15360], P(None, None, 'dp'), may hold values from -0.046875 to 0.046875
- down_input_factor: bfloat16 [15360, 64], P('dp'), may hold values from -0.046875 to 0.046875
- down_output_factor: bfloat16 [64, 8192], P(None, 'mp'), may hold values from -0.0625 to 0.0625
- cotangent: bfloat16 [256, 8192], P('dp', 'mp'), may hold values from -6 to 6
Outputs:
- output: bfloat16 [256, 8192], P('dp', 'mp')
- input_grad: bfloat16 [256, 8192], P('dp', 'mp')
- grad_gate_up_lower: float32 [2, 8192, 64], P(None, 'mp')
- gate_up_output_factor_gradient: float32 [2, 64, 15360], P(None, None, 'dp')
- down_input_factor_gradient: float32 [15360, 64], P('dp')
- down_output_factor_gradient: float32 [64, 8192], P(None, 'mp')
All inputs are finite; a program needn't handle non-finite values.
Results may differ from a plain program's by a relative error of at most 0.0065.
Values may be sent and summed in bfloat16 or wider, within the bound.
No kernel may reach another device: no remote copies, remote signals or barrier semaphores. Data moves between devices by JAX's collectives and lax.ppermute only.
A program may use at most 64 MiB of HBM per device.

v0:
```python
import jax
import jax.numpy as jnp
from jax import lax
from jax.sharding import Mesh
from jax.sharding import PartitionSpec as P

MP = ("mp_0", "mp_1")


adapter_scale = 2.0


def sent_to_all(array, axis):
    length = lax.axis_size(axis)
    return lax.all_to_all(
        jnp.broadcast_to(array[None], (length, *array.shape)), axis, 0, 0, tiled=True
    )


def joined_along(parts, dim):
    shape = list(parts.shape[1:])
    shape[dim] *= parts.shape[0]
    return jnp.moveaxis(parts, 0, dim).reshape(shape)


def gathered_copies(array, axis, dim):
    parts = sent_to_all(array, axis)
    return joined_along(parts, dim)


def cut_along(array, dim, length):
    shape = array.shape
    parts = array.reshape(*shape[:dim], length, shape[dim] // length, *shape[dim + 1 :])
    return jnp.moveaxis(parts, dim, 0)


def piece_ends(length, count):
    hop = length // count
    if hop >= 8:
        hop -= hop % 8
    return [hop * k for k in range(1, count)]


def sum_in_order(parts, axes, turns):
    shape = [lax.axis_size(a) for a in axes]
    parts = parts.reshape(*shape, *parts.shape[1:])
    parts = parts.transpose(*turns, *range(len(axes), parts.ndim))
    parts = parts.reshape(-1, *parts.shape[len(axes) :])
    for k in turns:
        parts = lax.psum_scatter(parts, axes[k], scatter_dimension=0, tiled=True)
    return parts[0]


def sum_at_once(array, axes, dim):
    parts = cut_along(array, dim, lax.axis_size(axes))
    widest = max(range(1, max(2, parts.ndim - 1)), key=lambda d: parts.shape[d])
    count, finished = (len(axes), [])
    for first, section in enumerate(
        jnp.split(parts, piece_ends(parts.shape[widest], count), axis=widest)
    ):
        if section.size:
            turns = [(first + k) % count for k in range(count)]
            finished.append(sum_in_order(section, axes, turns))
    return jnp.concatenate(finished, axis=widest - 1)


def sum_at_owner(array, axis, dim):
    parts = cut_along(array, dim, lax.axis_size(axis))
    arrived = lax.all_to_all(parts, axis, split_axis=0, concat_axis=0, tiled=True)
    return arrived.sum(axis=0)


def over_copies(array, axis):
    return sent_to_all(array, axis).sum(axis=0)


def in_one(arrays, axis):
    ravelled, at, finished = (jnp.concatenate([a.reshape(-1) for a in arrays]), 0, [])
    so_far = over_copies(ravelled, axis)
    for a in arrays:
        finished.append(so_far[at : at + a.size].reshape(a.shape))
        at += a.size
    return tuple(finished)


def contract_trailing(left, right, matmul_precision=None):
    return lax.dot_general(
        left,
        right,
        (((1,), (1,)), ((), ())),
        preferred_element_type=jnp.float32,
        precision=matmul_precision,
    )


def contract_leading(left, right, matmul_precision=None):
    return lax.dot_general(
        left,
        right,
        (((0,), (0,)), ((), ())),
        preferred_element_type=jnp.float32,
        precision=matmul_precision,
    )


def per_device(
    tokens,
    gate_up_weight,
    down_weight,
    gate_up_input_factor,
    gate_up_output_factor,
    down_input_factor,
    down_output_factor,
    cotangent,
):
    single_float = jnp.float32
    product_precision = lax.Precision.DEFAULT
    tok_rows = tokens.shape[0]
    input_rows_full = gathered_copies(tokens, "dp", 0)
    total = input_rows_full.shape[0]
    mp_rows = total // lax.axis_size(MP)
    scale_factor = total ** (-0.5)
    mp_start = lax.axis_index(MP) * mp_rows
    dp_start = lax.axis_index("dp") * tok_rows
    low_part = jnp.einsum(
        "td,kdr->tkr", input_rows_full, gate_up_input_factor, preferred_element_type=single_float
    )
    upper_widened = gate_up_output_factor.astype(single_float)
    term = jnp.einsum(
        "td,kdf->tkf", input_rows_full, gate_up_weight, preferred_element_type=single_float
    )
    low_slab = low_part
    term = term + adapter_scale * jnp.einsum("ubw,bwa->uba", low_slab, upper_widened)
    preactivation = sum_at_once(term, MP, 0)
    gate = preactivation[:, 0]
    upper = preactivation[:, 1]
    hidden_state = (jax.nn.silu(gate) * upper).astype(jnp.bfloat16)
    hidden_state_full = gathered_copies(hidden_state, MP, 0)
    low_down_part = jnp.dot(
        hidden_state_full, down_input_factor, preferred_element_type=single_float
    )
    down_widened_rows = down_output_factor.astype(single_float)
    term = jnp.dot(hidden_state_full, down_weight, preferred_element_type=single_float)
    low_slab = low_down_part
    term = term + adapter_scale * jnp.dot(low_slab, down_widened_rows)
    output = sum_at_owner(term, "dp", 0)
    output = output.astype(jnp.bfloat16)
    cot_all = gathered_copies(cotangent, "dp", 0)
    coeff_part = contract_leading(
        low_down_part, cot_all.astype(single_float), matmul_precision=product_precision
    )
    backward_down_rows = over_copies(contract_trailing(cot_all, down_output_factor), MP).astype(
        jnp.bfloat16
    )
    hidden_state_gradient = lax.psum_scatter(
        contract_trailing(cot_all, down_weight), MP, scatter_dimension=0, tiled=True
    )
    backward_row_block = lax.dynamic_slice_in_dim(backward_down_rows, mp_start, mp_rows, 0)
    hidden_state_gradient = hidden_state_gradient + adapter_scale * contract_trailing(
        backward_row_block, down_input_factor
    )
    down_input_factor_gradient = (
        adapter_scale * scale_factor * contract_leading(hidden_state_full, backward_down_rows)
    )
    sigma = jax.nn.sigmoid(gate)
    gate_back = hidden_state_gradient * upper * sigma * (1.0 + gate * (1.0 - sigma))
    up_back = hidden_state_gradient * gate * sigma
    pre_back = jnp.stack([gate_back, up_back], axis=1).astype(jnp.bfloat16)
    back_all = gathered_copies(pre_back, MP, 0)
    upper_partial = jnp.einsum("tkr,tkf->krf", low_part, back_all.astype(single_float))
    gate_up_output_factor_gradient = adapter_scale * scale_factor * lax.psum(upper_partial, MP)
    back_low_part = jnp.einsum(
        "tkf,krf->tkr", back_all, gate_up_output_factor, preferred_element_type=single_float
    )
    back_low_sum, down_coefficient = in_one((back_low_part, coeff_part), "dp")
    down_output_factor_gradient = adapter_scale * scale_factor * down_coefficient
    backward_lower_rows = back_low_sum.astype(jnp.bfloat16)
    grad_gate_up_lower = (
        adapter_scale
        * scale_factor
        * jnp.einsum(
            "qi,qps->pis", input_rows_full, backward_lower_rows, preferred_element_type=single_float
        )
    )
    input_total_sum = sum_at_owner(
        jnp.einsum("tkf,kdf->td", back_all, gate_up_weight, preferred_element_type=single_float),
        "dp",
        0,
    )
    low_rows_back = lax.dynamic_slice_in_dim(backward_lower_rows, dp_start, tok_rows, 0)
    input_total_sum = input_total_sum + adapter_scale * jnp.einsum(
        "tkr,kdr->td", low_rows_back, gate_up_input_factor, preferred_element_type=single_float
    )
    input_grad = input_total_sum.astype(jnp.bfloat16)
    return (
        output,
        input_grad,
        grad_gate_up_lower,
        gate_up_output_factor_gradient,
        down_input_factor_gradient,
        down_output_factor_gradient,
    )


def solution(mesh):
    torus = Mesh(mesh.devices.reshape(mesh.shape["dp"], 4, 4), ("dp", "mp_0", "mp_1"))
    in_specs = (
        P("dp", MP),
        P(None, MP, "dp"),
        P("dp", MP),
        P(None, MP, None),
        P(None, None, "dp"),
        P("dp", None),
        P(None, MP),
        P("dp", MP),
    )
    out_specs = (
        P("dp", MP),
        P("dp", MP),
        P(None, MP, None),
        P(None, None, "dp"),
        P("dp", None),
        P(None, MP),
    )
    return jax.shard_map(
        per_device, mesh=torus, in_specs=in_specs, out_specs=out_specs, check_vma=False
    )
```

profile of v0, /device:TPU:0, one launch (start us, length us, event | category | flops | bytes accessed | tf_op | source)
XLA Modules:
  0.0 345.4 jit_solution(7605972328173418897)
XLA Ops:
  9.0 11.7 %all_to_all.41 = bf16[8,32,512]{2,1,0:T(8,128)(2,1)S(1)} all-to-all(bf16[8,32,512]{2,1,0:T(8,128)(2,1)S(1)} %broadcast_in_dim.12), channel_id=1, replica_groups=mesh['dp'=8,'mp_0'=4,'mp_1'=4] {'dp'}, dimensions={0} | all-to-all | bytes 524288 | tf_op jit(solution)/shard_map/all_to_all | solution.py:15
  20.7 3.4 fusion.22
  25.0 1.6 fusion.19
  26.6 1.4 copy.44
  28.1 3.0 copy.52
  31.8 9.9 %all_to_all.42 = bf16[8,32,512]{2,1,0:T(8,128)(2,1)S(1)} all-to-all(bf16[8,32,512]{2,1,0:T(8,128)(2,1)S(1)} %broadcast_in_dim.14), channel_id=1, replica_groups=mesh['dp'=8,'mp_0'=4,'mp_1'=4] {'dp'}, dimensions={0} | all-to-all | bytes 524288 | tf_op jit(solution)/shard_map/all_to_all | solution.py:15
  41.8 2.0 fusion.25
  43.8 14.1 %reduce-scatter.9.cloned.1.call-done = f32[4,8,2,1920]{3,1,2,0:T(8,128)} async-done(((f32[16,8,2,1920]{3,1,2,0:T(8,128)}), f32[4,8,2,1920]{3,1,2,0:T(8,128)}) %reduce-scatter.9.cloned.1.call-update) | async-done | bytes 491536 | tf_op jit(solution)/shard_map/reduce_scatter | solution.py:50
  59.3 5.5 %all-to-all-start.4 = ((f32[16,256,64]{1,2,0:T(8,128)}), f32[16,256,64]{1,2,0:T(8,128)}, u32[]{:S(2)}, u32[]{:S(2)}) async-start(f32[16,256,64]{1,2,0:T(8,128)} %broadcast_in_dim.15), calls=%async_computation.8 | async-start | bytes 2097152 | tf_op jit(solution)/shard_map/all_to_all | solution.py:15
  64.8 32.6 %reduce-scatter.5.cloned.1.call-done = f32[4,8,2,1920]{3,1,2,0:T(8,128)} async-done(((f32[16,8,2,1920]{3,1,2,0:T(8,128)}), f32[4,8,2,1920]{3,1,2,0:T(8,128)}) %reduce-scatter.5.cloned.1.call-update) | async-done | bytes 491536 | tf_op jit(solution)/shard_map/reduce_scatter | solution.py:50
  99.9 46.6 %all-reduce.6.cloned.1.call-done = f32[256,1920]{1,0:T(8,128)} async-done(((f32[256,1920]{1,0:T(8,128)}), f32[256,1920]{1,0:T(8,128)}) %all-reduce.6.cloned.1.call-update) | async-done | bytes 1966096
  146.5 2.1 fusion.15
  149.6 4.9 %all-to-all-start.1 = ((bf16[16,16,1920]{2,1,0:T(8,128)(2,1)}), bf16[16,16,1920]{2,1,0:T(8,128)(2,1)S(1)}, u32[]{:S(2)}, u32[]{:S(2)}) async-start(bf16[16,16,1920]{2,1,0:T(8,128)(2,1)} %broadcast_in_dim.13), calls=%async_computation.5 | async-start | bytes 1966080 | tf_op jit(solution)/shard_map/all_to_all | solution.py:15
  154.6 1.5 pad_maximum_fusion.2
  156.1 14.7 %all-to-all-done.1 = bf16[16,16,1920]{2,1,0:T(8,128)(2,1)S(1)} async-done(((bf16[16,16,1920]{2,1,0:T(8,128)(2,1)}), bf16[16,16,1920]{2,1,0:T(8,128)(2,1)S(1)}, u32[]{:S(2)}, u32[]{:S(2)}) %all-to-all-start.1) | async-done | bytes 983072 | tf_op jit(solution)/shard_map/all_to_all | solution.py:15
  170.8 2.3 broadcast_in_dim.16
  173.1 4.4 %all-to-all-start.5 = ((bf16[16,16,2,1920]{3,1,2,0:T(8,128)(2,1)}), bf16[16,16,2,1920]{3,1,2,0:T(8,128)(2,1)}, u32[]{:S(2)}, u32[]{:S(2)}) async-start(bf16[16,16,2,1920]{3,1,2,0:T(8,128)(2,1)} %broadcast_in_dim.16), calls=%async_computation.9 | async-start | bytes 3932160 | tf_op jit(solution)/shard_map/all_to_all | solution.py:15
  177.5 1.4 fusion.24
  180.0 1.5 convolution_add_fusion
  181.5 22.5 %all-to-all-done.5 = bf16[16,16,2,1920]{3,1,2,0:T(8,128)(2,1)} async-done(((bf16[16,16,2,1920]{3,1,2,0:T(8,128)(2,1)}), bf16[16,16,2,1920]{3,1,2,0:T(8,128)(2,1)}, u32[]{:S(2)}, u32[]{:S(2)}) %all-to-all-start.5) | async-done | bytes 1966112 | tf_op jit(solution)/shard_map/all_to_all | solution.py:15
  204.0 4.3 %all-to-all-start.2 = ((f32[8,32,512]{2,1,0:T(8,128)}), f32[8,32,512]{2,1,0:T(8,128)}, u32[]{:S(2)}, u32[]{:S(2)}) async-start(f32[8,32,512]{2,1,0:T(8,128)} %bitcast.110), calls=%async_computation.6 | async-start | bytes 1048576 | tf_op jit(solution)/shard_map/all_to_all | solution.py:69
  208.2 1.7 copy.45
  214.5 4.7 %fusion.3 = f32[8,32,512]{2,1,0:T(8,128)} fusion(bf16[8,32,1920,2]{2,1,0,3:T(8,128)(2,1)} %bitcast.96, bf16[2,512,1920]{2,1,0:T(8,128)(2,1)} %param.9), kind=kOutput, calls=%fused_computation.6 | convolution fusion | flops 1006632960 | bytes 6422528 | tf_op jit(solution)/shard_map/tkf,kdf->td/dot_general | solution.py:186
  219.3 4.8 %all-to-all-start.6 = ((f32[8,32,512]{2,1,0:T(8,128)}), f32[8,32,512]{2,1,0:T(8,128)}, u32[]{:S(2)}, u32[]{:S(2)}) async-start(f32[8,32,512]{2,1,0:T(8,128)} %fusion.3), calls=%async_computation.10 | async-start | bytes 1048576 | tf_op jit(solution)/shard_map/all_to_all | solution.py:69
  225.0 9.4 %all-to-all-done.6 = f32[8,32,512]{2,1,0:T(8,128)} async-done(((f32[8,32,512]{2,1,0:T(8,128)}), f32[8,32,512]{2,1,0:T(8,128)}, u32[]{:S(2)}, u32[]{:S(2)}) %all-to-all-start.6) | async-done | bytes 524320 | tf_op jit(solution)/shard_map/all_to_all | solution.py:69
  234.5 2.4 broadcast_in_dim.17
  236.9 4.5 %all-to-all-start.7 = ((f32[8,1,65536]{2,1,0:T(1,128)}), f32[8,1,65536]{2,1,0:T(1,128)}, u32[]{:S(2)}, u32[]{:S(2)}) async-start(f32[8,1,65536]{2,1,0:T(1,128)} %broadcast_in_dim.17), calls=%async_computation.11 | async-start | bytes 4194304 | tf_op jit(solution)/shard_map/all_to_all | solution.py:15
  241.6 2.9 fusion.27
  245.7 1.7 reduce_sum.36
  248.4 81.9 %all-reduce.4.cloned.1.call-done = f32[2,64,1920]{2,1,0:T(8,128)} async-done(((f32[2,64,1920]{2,1,0:T(8,128)}), f32[2,64,1920]{2,1,0:T(8,128)}) %all-reduce.4.cloned.1.call-update) | async-done | bytes 983056 | tf_op jit(solution)/shard_map/psum | solution.py:171
  330.3 2.2 broadcast_multiply_fusion
  332.5 3.2 reduce_sum.39
  (70 shorter events, 18.6 us)
Async XLA Ops:
  8.0 33.8 %copy-start = (bf16[1920,512]{1,0:T(8,128)(2,1)S(1)}, bf16[1920,512]{1,0:T(8,128)(2,1)}, u32[]{:S(2)}) copy-start(bf16[1920,512]{1,0:T(8,128)(2,1)} %param.10) | copy-start | bytes 5898244
  8.0 49.9 %reduce-scatter.9.cloned.1.call-start = ((), (), s32[]{:S(2)}) async-start(), calls=%async_computation.14 | async-start | bytes 2457600 | tf_op jit(solution)/shard_map/reduce_scatter | solution.py:50
  20.7 3.4 copy-start.6
  20.7 3.6 %copy-start.2 = (bf16[2,64,1920]{2,1,0:T(8,128)(2,1)S(1)}, bf16[2,64,1920]{2,1,0:T(8,128)(2,1)}, u32[]{:S(2)}) copy-start(bf16[2,64,1920]{2,1,0:T(8,128)(2,1)} %param.12) | copy-start | bytes 1474564
  24.3 0.7 copy-start.4
  28.0 69.3 %reduce-scatter.5.cloned.1.call-start = ((), (), s32[]{:S(2)}) async-start(), calls=%async_computation.12 | async-start | bytes 2457600 | tf_op jit(solution)/shard_map/reduce_scatter | solution.py:50
  31.1 0.8 copy-start.12
  31.1 115.4 %all-reduce.6.cloned.1.call-start = ((), (), s32[]{:S(2)}) async-start(), calls=%async_computation.17 | async-start | bytes 3932160
  43.8 14.2 %copy-start.8 = (bf16[64,512]{1,0:T(8,128)(2,1)S(1)}, bf16[64,512]{1,0:T(8,128)(2,1)}, u32[]{:S(2)}) copy-start(bf16[64,512]{1,0:T(8,128)(2,1)} %param.14) | copy-start | bytes 196612
  43.8 102.7 %reduce-scatter.11.cloned.1.call-start = ((), (), s32[]{:S(2)}) async-start(), calls=%async_computation.15 | async-start | bytes 614400 | tf_op jit(solution)/shard_map/reduce_scatter | solution.py:50
  58.2 39.2 %copy-start.13 = (u32[128]{0:T(128)S(1)}, u32[128]{0:T(128)}, u32[]{:S(2)}) copy-start(u32[128]{0:T(128)} %constant.41) | copy-start | bytes 1540
  59.2 87.3 %copy-start.9 = (bf16[1920,64]{0,1:T(8,128)(2,1)S(1)}, bf16[1920,64]{0,1:T(8,128)(2,1)}, u32[]{:S(2)}) copy-start(bf16[1920,64]{0,1:T(8,128)(2,1)} %param.13) | copy-start | bytes 737284
  59.3 39.4 %all-to-all-start.4 = ((f32[16,256,64]{1,2,0:T(8,128)}), f32[16,256,64]{1,2,0:T(8,128)}, u32[]{:S(2)}, u32[]{:S(2)}) async-start(f32[16,256,64]{1,2,0:T(8,128)} %broadcast_in_dim.15), calls=%async_computation.8 | async-start | bytes 2097152 | tf_op jit(solution)/shard_map/all_to_all | solution.py:15
  64.7 81.8 %reduce-scatter.7.cloned.1.call-start = ((), (), s32[]{:S(2)}) async-start(), calls=%async_computation.13 | async-start | bytes 614400 | tf_op jit(solution)/shard_map/reduce_scatter | solution.py:50
  99.9 49.7 %copy-start.10 = (bf16[256,64]{0,1:T(8,128)(2,1)}, bf16[256,64]{0,1:T(8,128)(2,1)S(1)}, u32[]{:S(2)}) copy-start(bf16[256,64]{0,1:T(8,128)(2,1)S(1)} %reduce_sum.37) | copy-start | bytes 98308
  149.6 21.1 %all-to-all-start.1 = ((bf16[16,16,1920]{2,1,0:T(8,128)(2,1)}), bf16[16,16,1920]{2,1,0:T(8,128)(2,1)S(1)}, u32[]{:S(2)}, u32[]{:S(2)}) async-start(bf16[16,16,1920]{2,1,0:T(8,128)(2,1)} %broadcast_in_dim.13), calls=%async_computation.5 | async-start | bytes 1966080 | tf_op jit(solution)/shard_map/all_to_all | solution.py:15
  173.1 30.9 %all-to-all-start.5 = ((bf16[16,16,2,1920]{3,1,2,0:T(8,128)(2,1)}), bf16[16,16,2,1920]{3,1,2,0:T(8,128)(2,1)}, u32[]{:S(2)}, u32[]{:S(2)}) async-start(bf16[16,16,2,1920]{3,1,2,0:T(8,128)(2,1)} %broadcast_in_dim.16), calls=%async_computation.9 | async-start | bytes 3932160 | tf_op jit(solution)/shard_map/all_to_all | solution.py:15
  204.0 15.3 %all-to-all-start.2 = ((f32[8,32,512]{2,1,0:T(8,128)}), f32[8,32,512]{2,1,0:T(8,128)}, u32[]{:S(2)}, u32[]{:S(2)}) async-start(f32[8,32,512]{2,1,0:T(8,128)} %bitcast.110), calls=%async_computation.6 | async-start | bytes 1048576 | tf_op jit(solution)/shard_map/all_to_all | solution.py:69
  208.2 3.0 copy-start.3
  210.0 1.3 copy-start.1
  219.3 15.2 %all-to-all-start.6 = ((f32[8,32,512]{2,1,0:T(8,128)}), f32[8,32,512]{2,1,0:T(8,128)}, u32[]{:S(2)}, u32[]{:S(2)}) async-start(f32[8,32,512]{2,1,0:T(8,128)} %fusion.3), calls=%async_computation.10 | async-start | bytes 1048576 | tf_op jit(solution)/shard_map/all_to_all | solution.py:69
  236.9 4.7 %copy-start.5 = (f32[256,128]{0,1:S(1)}, f32[256,128]{0,1}, u32[]{:S(2)}) copy-start(f32[256,128]{0,1} %copy-done.4) | copy-start | bytes 393220
  236.9 95.6 %all-to-all-start.7 = ((f32[8,1,65536]{2,1,0:T(1,128)}), f32[8,1,65536]{2,1,0:T(1,128)}, u32[]{:S(2)}, u32[]{:S(2)}) async-start(f32[8,1,65536]{2,1,0:T(1,128)} %broadcast_in_dim.17), calls=%async_computation.11 | async-start | bytes 4194304 | tf_op jit(solution)/shard_map/all_to_all | solution.py:15
  241.4 3.2 copy-start.11
  241.4 88.9 %all-reduce.4.cloned.1.call-start = ((), (), s32[]{:S(2)}) async-start(), calls=%async_computation.16 | async-start | bytes 1966080 | tf_op jit(solution)/shard_map/psum | solution.py:171
  332.5 4.9 %copy-start.7 = (bf16[2,512,64]{1,2,0:T(8,128)(2,1)S(1)}, bf16[2,512,64]{1,2,0:T(8,128)(2,1)}, u32[]{:S(2)}) copy-start(bf16[2,512,64]{1,2,0:T(8,128)(2,1)} %param.11) | copy-start | bytes 393220
Sparse Core Ops, SparseCore 0:
  28.2 29.7 reduce-scatter.8
  60.3 36.9 reduce-scatter.4
  99.7 21.1 reduce-scatter.10
  123.2 22.1 reduce-scatter.6
Sparse Core Ops, SparseCore 1:
  43.9 102.6 all-reduce.5
  245.8 84.5 all-reduce.3
where the time goes:
time: 347 us; the launch traced here: 345 us
  waiting for transfers between devices  222 us (64%)
  starting transfers between devices  28.8 us (8%)
  matrix products  23.7 us (7%)
  blocking collectives  21.6 us (6%)
  local copies, waits for them, and re-layouts  21.4 us (6%)
  between operations  16.2 us (5%)
  other arithmetic  12 us (3%)
    psum x1, waiting for transfers between devices, per_device(): lax.psum(upper_partial, MP)  81.9 us
    unnamed x7, waiting for transfers between devices  46.7 us
    reduce_scatter x4, waiting for transfers between devices, sum_in_order(): parts = lax.psum_scatter(parts, axes[k], scatter_dimension=0, tiled=True)  46.6 us
    all_to_all x4, waiting for transfers between devices, sent_to_all(): lax.all_to_all(jnp.broadcast_to(array[None], (length, *array.shape)), axi...  37.1 us
    all_to_all x2, blocking collectives, sent_to_all(): lax.all_to_all(jnp.broadcast_to(array[None], (length, *array.shape)), axi...  21.6 us
    all_to_all x4, starting transfers between devices, sent_to_all(): lax.all_to_all(jnp.broadcast_to(array[None], (length, *array.shape)), axi...  19.3 us
    all_to_all x2, waiting for transfers between devices, sum_at_owner(): lax.all_to_all(parts, axis, split_axis=0, concat_axis=0, tiled=True)  9.43 us
    all_to_all x2, starting transfers between devices, sum_at_owner(): lax.all_to_all(parts, axis, split_axis=0, concat_axis=0, tiled=True)  9.07 us
  transfers between devices with their start and end apart: 12, of which 7 were waited for; matrix products, arithmetic and copies ran while one was open for 10% of the time, Pallas kernels for 0%

commit v1 on v0

v1 whole, which is shorter than its diff:
```python
import jax
import jax.numpy as jnp
from jax import lax
from jax.sharding import Mesh
from jax.sharding import PartitionSpec as P

F32 = jnp.float32
BF16 = jnp.bfloat16
adapter_scale = 2.0
CUT = 896


def shifted(x, axis, by):
    n = lax.axis_size(axis)
    return lax.ppermute(x, axis, [(i, (i + by) % n) for i in range(n)])


def other_core(x):
    return lax.ppermute(x, "dp", [(i, i ^ 1) for i in range(lax.axis_size("dp"))])


def to_chip(x, by):
    n = lax.axis_size("dp")
    return lax.ppermute(x, "dp", [(i, (i + 2 * by) % n) for i in range(n)])


def dot(a, b, dims=((1,), (0,))):
    return lax.dot_general(a, b, (dims, ((), ())), preferred_element_type=F32)


def gather_direct(x, axis):
    return jnp.stack([x, shifted(x, axis, -1), shifted(x, axis, 2), shifted(x, axis, 1)])


def gather_ring(x, axis):
    after, before = shifted(x, axis, -1), shifted(x, axis, 1)
    h = x.shape[-1] // 256 * 128
    a = shifted(before[..., :h], axis, 1)
    b = shifted(after[..., h:], axis, -1)
    return jnp.stack([x, after, jnp.concatenate([a, b], -1), before])


def gathered(x, first, second):
    g = gather_ring(gather_direct(x, first), second)
    if first == "y":
        g = g.transpose(1, 0, 2, 3)
    return g.reshape(256, x.shape[-1])


def sum_direct(x, axis):
    return (
        x[0].astype(F32)
        + shifted(x[1], axis, 1).astype(F32)
        + shifted(x[2], axis, 2).astype(F32)
        + shifted(x[3], axis, -1).astype(F32)
    )


def sum_ring(x, axis):
    h = x.shape[-1] // 256 * 128
    a = shifted(x[2][..., :h], axis, 1)
    b = shifted(x[2][..., h:], axis, -1)
    up = jnp.concatenate(
        [(x[1][..., :h].astype(F32) + a.astype(F32)).astype(BF16), x[1][..., h:]], -1
    )
    down = jnp.concatenate(
        [x[3][..., :h], (x[3][..., h:].astype(F32) + b.astype(F32)).astype(BF16)], -1
    )
    return x[0].astype(F32) + shifted(up, axis, 1).astype(F32) + shifted(down, axis, -1).astype(F32)


def scattered_sum(x, first, second):
    x = x.reshape(4, 4, 16, x.shape[-1])
    if first == "z":
        x = x.transpose(1, 0, 2, 3)
    return sum_direct(sum_direct(x, first).astype(BF16), second)


def per_device(
    tokens,
    gate_up_weight,
    down_weight,
    gate_up_input_factor,
    gate_up_output_factor,
    down_input_factor,
    down_output_factor,
    cotangent,
):
    scale = adapter_scale * 256 ** (-0.5)
    dp = lax.axis_index("dp")
    chip, core = dp // 2, dp % 2
    y, z = lax.axis_index("y"), lax.axis_index("z")

    mine = jnp.concatenate([tokens, cotangent], 1)
    pair = jnp.concatenate([mine, other_core(mine)], 0)
    near = jnp.concatenate([pair, to_chip(pair, -1), to_chip(pair, 2), to_chip(pair, 1)], 0)

    n = jnp.arange(256, dtype=jnp.int32)
    token_of_row = 64 * ((y + n // 64) % 4) + 16 * ((z + n // 16 % 4) % 4) + n % 16
    token_of_near = 64 * ((chip + n // 64) % 4) + 32 * (core ^ (n // 32 % 2)) + n % 32
    turn = (token_of_row[:, None] == token_of_near[None, :]).astype(BF16)
    rows = dot(turn, near).astype(BF16)
    x, c = rows[:, :512], rows[:, 512:]

    wg, wu = gate_up_weight[0], gate_up_weight[1]
    a_both = jnp.concatenate([gate_up_input_factor[0], gate_up_input_factor[1]], 1)
    low_part = dot(x, a_both)
    back_down_part = dot(c, down_output_factor, ((1,), (1,)))
    part_a = jnp.concatenate(
        [
            low_part,
            back_down_part,
            jnp.zeros((256, 64), F32),
            dot(x, wg[:, :CUT]),
            dot(x, wu[:, :CUT]),
            dot(c, down_weight[:CUT], ((1,), (1,))),
        ],
        1,
    ).astype(BF16)
    part_b = jnp.concatenate(
        [
            dot(x, wg[:, CUT:]),
            dot(x, wu[:, CUT:]),
            dot(c, down_weight[CUT:], ((1,), (1,))),
        ],
        1,
    ).astype(BF16)
    sum_a = scattered_sum(part_a, "y", "z")
    sum_b = scattered_sum(part_b, "z", "y")
    low, back_down = sum_a[:, :128], sum_a[:, 128:192].astype(BF16)

    def middle(gate, up, back, cols):
        bg = gate_up_output_factor[0][:, cols].astype(F32)
        bu = gate_up_output_factor[1][:, cols].astype(F32)
        gate = gate + adapter_scale * dot(low[:, :64], bg)
        up = up + adapter_scale * dot(low[:, 64:], bu)
        back = back + adapter_scale * dot(back_down, down_input_factor[cols], ((1,), (1,)))
        s = jax.nn.sigmoid(gate)
        hidden = (gate * s * up).astype(BF16)
        gate_back = (back * up * s * (1.0 + gate * (1.0 - s))).astype(BF16)
        up_back = (back * gate * s).astype(BF16)
        return hidden, gate_back, up_back

    w = CUT
    parts_a = middle(
        sum_a[:, 256 : 256 + w], sum_a[:, 256 + w : 256 + 2 * w], sum_a[:, 256 + 2 * w :], slice(0, w)
    )
    v = 1920 - CUT
    parts_b = middle(sum_b[:, :v], sum_b[:, v : 2 * v], sum_b[:, 2 * v :], slice(w, 1920))
    all_a = gathered(
        jnp.concatenate(
            [low.astype(BF16), back_down, jnp.zeros((16, 64), BF16), *parts_a], 1
        ),
        "z",
        "y",
    )
    all_b = gathered(jnp.concatenate(parts_b, 1), "y", "z")
    low_all, back_down_all = all_a[:, :128], all_a[:, 128:192]
    hidden_a, gate_a, up_a = (all_a[:, 256 + i * w : 256 + (i + 1) * w] for i in range(3))
    hidden_b, gate_b, up_b = (all_b[:, i * v : (i + 1) * v] for i in range(3))

    t = ((1,), (1,))
    bo = gate_up_output_factor
    back_low_part = jnp.concatenate(
        [
            dot(gate_a, bo[0][:, :w], t) + dot(gate_b, bo[0][:, w:], t),
            dot(up_a, bo[1][:, :w], t) + dot(up_b, bo[1][:, w:], t),
        ],
        1,
    )
    low_down_part = dot(hidden_a, down_input_factor[:w]) + dot(hidden_b, down_input_factor[w:])
    out_part = (
        dot(hidden_a, down_weight[:w])
        + dot(hidden_b, down_weight[w:])
        + adapter_scale * dot(low_down_part, down_output_factor.astype(F32))
    )
    grad_part = (
        dot(gate_a, wg[:, :w], t)
        + dot(gate_b, wg[:, w:], t)
        + dot(up_a, wu[:, :w], t)
        + dot(up_b, wu[:, w:], t)
    )
    sums = jnp.concatenate(
        [back_low_part, low_down_part, jnp.zeros((256, 64), F32), out_part, grad_part], 1
    ).astype(BF16)
    sums = dot(turn, sums, ((0,), (0,))).astype(BF16).reshape(4, 2, 32, 1280)
    sums = (sums[:, 0].astype(F32) + other_core(sums[:, 1]).astype(F32)).astype(BF16)
    small, large = sums[..., :256], sums[..., 256:]
    small_sum, large_sum = small.astype(F32), large[0].astype(F32)
    for k in (1, 3, 2):
        sent = jnp.concatenate([large[k]] + [small[j] for j in range(4)], 1)
        got = to_chip(sent, k)
        large_sum = large_sum + got[:, :1024].astype(F32)
        theirs = [got[:, 1024 + 256 * j : 1280 + 256 * j] for j in range(4)]
        small_sum = small_sum + jnp.stack([theirs[(j + k) % 4] for j in range(4)]).astype(F32)
    small_sum = small_sum.astype(BF16)
    small_all = jnp.stack([small_sum, other_core(small_sum)], 1).reshape(256, 256)
    back_low_all, low_down_all = small_all[:, :128], small_all[:, 128:192]

    output = large_sum[:, :512].astype(BF16)
    back_low = small_sum[0][:, :128]
    input_grad = (large_sum[:, 512:] + adapter_scale * dot(back_low, a_both, t)).astype(BF16)
    lower = scale * dot(near[:, :512], back_low_all, ((0,), (0,)))
    grad_gate_up_lower = jnp.stack([lower[:, :64], lower[:, 64:]])
    down_output_factor_gradient = scale * dot(low_down_all, near[:, 512:], ((0,), (0,)))
    o = ((0,), (0,))
    gate_up_output_factor_gradient = scale * jnp.stack(
        [
            jnp.concatenate([dot(low_all[:, :64], gate_a, o), dot(low_all[:, :64], gate_b, o)], 1),
            jnp.concatenate([dot(low_all[:, 64:], up_a, o), dot(low_all[:, 64:], up_b, o)], 1),
        ]
    )
    down_input_factor_gradient = scale * jnp.concatenate(
        [dot(hidden_a, back_down_all, o), dot(hidden_b, back_down_all, o)], 0
    )
    return (
        output,
        input_grad,
        grad_gate_up_lower,
        gate_up_output_factor_gradient,
        down_input_factor_gradient,
        down_output_factor_gradient,
    )


def solution(mesh):
    torus = Mesh(mesh.devices.reshape(mesh.shape["dp"], 4, 4), ("dp", "y", "z"))
    mp = ("y", "z")
    in_specs = (
        P("dp", mp),
        P(None, mp, "dp"),
        P("dp", mp),
        P(None, mp, None),
        P(None, None, "dp"),
        P("dp", None),
        P(None, mp),
        P("dp", mp),
    )
    out_specs = (
        P("dp", mp),
        P("dp", mp),
        P(None, mp, None),
        P(None, None, "dp"),
        P("dp", None),
        P(None, mp),
    )
    return jax.shard_map(
        per_device, mesh=torus, in_specs=in_specs, out_specs=out_specs, check_vma=False
    )
```

time: 347 us -> 141 us (0.41)
  waiting for transfers between devices: 222 us -> 41.3 us
  starting transfers between devices: 28.8 us -> 51.7 us
  blocking collectives: 21.6 us -> 0 us
  between operations: 16.2 us -> 1.54 us
  local copies, waits for them, and re-layouts: 21.4 us -> 10.1 us
  other arithmetic: 12 us -> 4.12 us
  matrix products: 23.7 us -> 29.9 us
    psum x1 -> x0, waiting for transfers between devices: 81.9 us -> none  [per_device(): lax.psum(upper_partial, MP)]
    ppermute x0 -> x35, starting transfers between devices: none -> 51.7 us  [the longest x26 43.2 us: shifted(): return lax.ppermute(x, axis, [(i, (i + by) % n) for i in range(n)])]
    unnamed x7 -> x0, waiting for transfers between devices: 46.7 us -> none
    reduce_scatter x4 -> x0, waiting for transfers between devices: 46.6 us -> none  [sum_in_order(): parts = lax.psum_scatter(parts, axes[k], scatter_dimension=0, tiled=True)]
    all_to_all x6 -> x0, waiting for transfers between devices: 46.6 us -> none  [the longest x4 37.1 us: sent_to_all(): lax.all_to_all(jnp.broadcast_to(array[None], (length, *array.shape)), axi...]
    ppermute x0 -> x35, waiting for transfers between devices: none -> 41.3 us  [the longest x26 26.3 us: shifted(): return lax.ppermute(x, axis, [(i, (i + by) % n) for i in range(n)])]
    all_to_all x6 -> x0, starting transfers between devices: 28.4 us -> none  [the longest x4 19.3 us: sent_to_all(): lax.all_to_all(jnp.broadcast_to(array[None], (length, *array.shape)), axi...]
    all_to_all x2 -> x0, blocking collectives: 21.6 us -> none  [sent_to_all(): lax.all_to_all(jnp.broadcast_to(array[None], (length, *array.shape)), axi...]
  transfers between devices with their start and end apart: 12 -> 35, of which waited for: 7 -> 12; matrix products, arithmetic and copies ran while one was open for 10% -> 10% of each run, Pallas kernels for 0% -> 0%
where the time goes in v1:
time: 141 us; the launch traced here: 139 us
  starting transfers between devices  51.7 us (37%)
  waiting for transfers between devices  41.3 us (29%)
  matrix products  29.9 us (21%)
  local copies, waits for them, and re-layouts  10.1 us (7%)
  other arithmetic  4.12 us (3%)
  between operations  1.54 us (1%)
    ppermute x26, starting transfers between devices, shifted(): return lax.ppermute(x, axis, [(i, (i + by) % n) for i in range(n)])  43.2 us
    dot_general x38, matrix products, dot(): return lax.dot_general(a, b, (dims, ((), ())), preferred_element_type=F32)  29.9 us
    ppermute x26, waiting for transfers between devices, shifted(): return lax.ppermute(x, axis, [(i, (i + by) % n) for i in range(n)])  26.3 us
    ppermute x6, waiting for transfers between devices, to_chip(): return lax.ppermute(x, 'dp', [(i, (i + 2 * by) % n) for i in range(n)])  14.9 us
    ppermute x6, starting transfers between devices, to_chip(): return lax.ppermute(x, 'dp', [(i, (i + 2 * by) % n) for i in range(n)])  8.23 us
    squeeze x1, local copies, waits for them, and re-layouts, per_device(): wg, wu = (gate_up_weight[0], gate_up_weight[1])  3.78 us
  transfers between devices with their start and end apart: 35, of which 12 were waited for; matrix products, arithmetic and copies ran while one was open for 10% of the time, Pallas kernels for 0%

profile of v1, /device:TPU:0, one launch (start us, length us, event | category | flops | bytes accessed | tf_op | source)
XLA Modules:
  0.0 138.7 jit_solution(16823811567366365289)
XLA Ops:
  2.3 3.8 %slice_bitcast_fusion.1 = (bf16[512,1920]{1,0:T(8,128)(2,1)}, bf16[512,1920]{1,0:T(8,128)(2,1)S(1)}) fusion(bf16[2,512,1920]{2,1,0:T(8,128)(2,1)} %param.9), kind=kLoop, calls=%fused_computation.2 | loop fusion | bytes 7864320 | tf_op jit(solution)/shard_map/squeeze | solution.py:105
  6.3 2.9 %collective-permute-start.1 = (bf16[64,1024]{1,0:T(8,128)(2,1)S(1)}, bf16[64,1024]{1,0:T(8,128)(2,1)S(1)}, u32[]{:S(2)}, u32[]{:S(2)}) collective-permute-start(bf16[64,1024]{1,0:T(8,128)(2,1)S(1)} %pad_maximum_fusion.5), channel_id=1, source_target_pairs={{0,96},{16,112},{32,0},{48,16},{64,32},{80,48},{96,64},{112,80},{1... | collective-permute-start | bytes 393224 | tf_op jit(solution)/shard_map/ppermute | solution.py:24
  11.0 4.4 %collective-permute-done.1 = bf16[64,1024]{1,0:T(8,128)(2,1)S(1)} collective-permute-done((bf16[64,1024]{1,0:T(8,128)(2,1)S(1)}, bf16[64,1024]{1,0:T(8,128)(2,1)S(1)}, u32[]{:S(2)}, u32[]{:S(2)}) %collective-permute-start.1) | collective-permute-done | bytes 131104 | tf_op jit(solution)/shard_map/ppermute | solution.py:24
  15.4 1.8 %collective-permute-done.2 = bf16[64,1024]{1,0:T(8,128)(2,1)S(1)} collective-permute-done((bf16[64,1024]{1,0:T(8,128)(2,1)S(1)}, bf16[64,1024]{1,0:T(8,128)(2,1)S(1)}, u32[]{:S(2)}, u32[]{:S(2)}) %collective-permute-start.2) | collective-permute-done | bytes 131104 | tf_op jit(solution)/shard_map/ppermute | solution.py:24
  17.2 2.0 %collective-permute-done.3 = bf16[64,1024]{1,0:T(8,128)(2,1)S(1)} collective-permute-done((bf16[64,1024]{1,0:T(8,128)(2,1)S(1)}, bf16[64,1024]{1,0:T(8,128)(2,1)S(1)}, u32[]{:S(2)}, u32[]{:S(2)}) %collective-permute-start.3) | collective-permute-done | bytes 131104 | tf_op jit(solution)/shard_map/ppermute | solution.py:24
  23.7 1.3 convolution_convert_fusion.1
  27.9 2.2 %concatenate.66 = bf16[256,2944]{1,0:T(8,128)(2,1)S(1)} concatenate(bf16[256,128]{1,0:T(8,128)(2,1)S(1)} %copy.22, bf16[256,64]{1,0:T(8,128)(2,1)S(1)} %copy.23, bf16[256,64]{1,0:T(8,128)(2,1)S(1)} %broadcast.310, bf16[256,896]{1,0:T(8,128)(2,1)S(1)} %copy-done.20, bf16[256,896]{1,0:T(8,128)(2,1)S(1)} %convolution_convert_fusion.6, bf16[256,896]{1,0:T(8,128)(2,1)} %convolution_convert_fusion.5), dimensions={1} | concatenate | bytes 3014656 | tf_op jit(solution)/shard_map/concatenate | solution.py:109
  30.2 3.1 %collective-permute-start.6 = (bf16[4,16,2944]{2,1,0:T(8,128)(2,1)S(1)}, bf16[4,16,2944]{2,1,0:T(8,128)(2,1)S(1)}, u32[]{:S(2)}, u32[]{:S(2)}) collective-permute-start(bf16[4,16,2944]{2,1,0:T(8,128)(2,1)S(1)} %bitcast.221), channel_id=1, source_target_pairs={{0,12},{4,0},{8,4},{12,8},{1,13},{5,1},{9,5},{13,9},{2,14},{6,2},{... | collective-permute-start | bytes 1130504 | tf_op jit(solution)/shard_map/ppermute | solution.py:15
  35.1 4.1 %collective-permute-start.19 = (bf16[4,16,3072]{2,1,0:T(8,128)(2,1)S(1)}, bf16[4,16,3072]{2,1,0:T(8,128)(2,1)S(1)}, u32[]{:S(2)}, u32[]{:S(2)}) collective-permute-start(bf16[4,16,3072]{2,1,0:T(8,128)(2,1)S(1)} %get-tuple-element.11), channel_id=1, source_target_pairs={{0,3},{1,0},{2,1},{3,2},{4,7},{5,4},{6,5},{7,6},{8,11},{9,8},{10,9... | collective-permute-start | bytes 1179656 | tf_op jit(solution)/shard_map/ppermute | solution.py:15
  39.2 10.3 %collective-permute-done.6 = bf16[4,16,2944]{2,1,0:T(8,128)(2,1)S(1)} collective-permute-done((bf16[4,16,2944]{2,1,0:T(8,128)(2,1)S(1)}, bf16[4,16,2944]{2,1,0:T(8,128)(2,1)S(1)}, u32[]{:S(2)}, u32[]{:S(2)}) %collective-permute-start.6) | collective-permute-done | bytes 376864 | tf_op jit(solution)/shard_map/ppermute | solution.py:15
  49.6 1.9 %collective-permute-start.17 = (bf16[4,16,3072]{2,1,0:T(8,128)(2,1)S(1)}, bf16[4,16,3072]{2,1,0:T(8,128)(2,1)S(1)}, u32[]{:S(2)}, u32[]{:S(2)}) collective-permute-start(bf16[4,16,3072]{2,1,0:T(8,128)(2,1)S(1)} %get-tuple-element.10), channel_id=1, source_target_pairs={{0,1},{1,2},{2,3},{3,0},{4,5},{5,6},{6,7},{7,4},{8,9},{9,10},{10,1... | collective-permute-start | bytes 1179656 | tf_op jit(solution)/shard_map/ppermute | solution.py:15
  51.5 1.8 %collective-permute-done.4 = bf16[4,16,2944]{2,1,0:T(8,128)(2,1)S(1)} collective-permute-done((bf16[4,16,2944]{2,1,0:T(8,128)(2,1)S(1)}, bf16[4,16,2944]{2,1,0:T(8,128)(2,1)S(1)}, u32[]{:S(2)}, u32[]{:S(2)}) %collective-permute-start.4) | collective-permute-done | bytes 376864 | tf_op jit(solution)/shard_map/ppermute | solution.py:15
  53.5 4.1 %collective-permute-start.9 = (bf16[16,2944]{1,0:T(8,128)(2,1)S(1)}, bf16[16,2944]{1,0:T(8,128)(2,1)S(1)}, u32[]{:S(2)}, u32[]{:S(2)}) collective-permute-start(bf16[16,2944]{1,0:T(8,128)(2,1)S(1)} %get-tuple-element.27), channel_id=1, source_target_pairs={{0,3},{1,0},{2,1},{3,2},{4,7},{5,4},{6,5},{7,6},{8,11},{9,8},{10,9... | collective-permute-start | bytes 282632 | tf_op jit(solution)/shard_map/ppermute | solution.py:15
  57.6 1.3 collective-permute-start.7
  58.9 4.8 %collective-permute-done.17 = bf16[4,16,3072]{2,1,0:T(8,128)(2,1)S(1)} collective-permute-done((bf16[4,16,3072]{2,1,0:T(8,128)(2,1)S(1)}, bf16[4,16,3072]{2,1,0:T(8,128)(2,1)S(1)}, u32[]{:S(2)}, u32[]{:S(2)}) %collective-permute-start.17) | collective-permute-done | bytes 393248 | tf_op jit(solution)/shard_map/ppermute | solution.py:15
  63.9 4.2 %collective-permute-start.22 = (bf16[16,3072]{1,0:T(8,128)(2,1)S(1)}, bf16[16,3072]{1,0:T(8,128)(2,1)S(1)}, u32[]{:S(2)}, u32[]{:S(2)}) collective-permute-start(bf16[16,3072]{1,0:T(8,128)(2,1)S(1)} %get-tuple-element.22), channel_id=1, source_target_pairs={{0,12},{4,0},{8,4},{12,8},{1,13},{5,1},{9,5},{13,9},{2,14},{6,2},{... | collective-permute-start | bytes 294920 | tf_op jit(solution)/shard_map/ppermute | solution.py:15
  70.7 2.9 %collective-permute-start.11 = (bf16[16,2944]{1,0:T(8,128)(2,1)S(1)}, bf16[16,2944]{1,0:T(8,128)(2,1)S(1)}, u32[]{:S(2)}, u32[]{:S(2)}) collective-permute-start(bf16[16,2944]{1,0:T(8,128)(2,1)S(1)} %concatenate.67), channel_id=1, source_target_pairs={{0,2},{1,3},{2,0},{3,1},{4,6},{5,7},{6,4},{7,5},{8,10},{9,11},{10,... | collective-permute-start | bytes 282632 | tf_op jit(solution)/shard_map/ppermute | solution.py:15
  73.6 2.2 %collective-permute-start.10 = (bf16[16,2944]{1,0:T(8,128)(2,1)S(1)}, bf16[16,2944]{1,0:T(8,128)(2,1)S(1)}, u32[]{:S(2)}, u32[]{:S(2)}) collective-permute-start(bf16[16,2944]{1,0:T(8,128)(2,1)S(1)} %concatenate.67), channel_id=1, source_target_pairs={{0,3},{1,0},{2,1},{3,2},{4,7},{5,4},{6,5},{7,6},{8,11},{9,8},{10,9... | collective-permute-start | bytes 282632 | tf_op jit(solution)/shard_map/ppermute | solution.py:15
  76.4 2.6 %collective-permute-start.25 = (bf16[16,3072]{1,0:T(8,128)(2,1)S(1)}, bf16[16,3072]{1,0:T(8,128)(2,1)S(1)}, u32[]{:S(2)}, u32[]{:S(2)}) collective-permute-start(bf16[16,3072]{1,0:T(8,128)(2,1)S(1)} %get-tuple-element.67), channel_id=1, source_target_pairs={{0,4},{4,8},{8,12},{12,0},{1,5},{5,9},{9,13},{13,1},{2,6},{6,10},{... | collective-permute-start | bytes 294920 | tf_op jit(solution)/shard_map/ppermute | solution.py:15
  80.3 1.6 %collective-permute-start.23 = (bf16[16,3072]{1,0:T(8,128)(2,1)S(1)}, bf16[16,3072]{1,0:T(8,128)(2,1)S(1)}, u32[]{:S(2)}, u32[]{:S(2)}) collective-permute-start(bf16[16,3072]{1,0:T(8,128)(2,1)S(1)} %get-tuple-element.67), channel_id=1, source_target_pairs={{0,12},{4,0},{8,4},{12,8},{1,13},{5,1},{9,5},{13,9},{2,14},{6,2},{... | collective-permute-start | bytes 294920 | tf_op jit(solution)/shard_map/ppermute | solution.py:15
  82.4 2.8 %collective-permute-start.13 = (bf16[4,16,2944]{2,1,0:T(8,128)(2,1)S(1)}, bf16[4,16,2944]{2,1,0:T(8,128)(2,1)S(1)}, u32[]{:S(2)}, u32[]{:S(2)}) collective-permute-start(bf16[4,16,2944]{2,1,0:T(8,128)(2,1)S(1)} %get-tuple-element.25), channel_id=1, source_target_pairs={{0,12},{4,0},{8,4},{12,8},{1,13},{5,1},{9,5},{13,9},{2,14},{6,2},{... | collective-permute-start | bytes 1130504 | tf_op jit(solution)/shard_map/ppermute | solution.py:15
  87.4 4.8 %collective-permute-done.13 = bf16[4,16,2944]{2,1,0:T(8,128)(2,1)S(1)} collective-permute-done((bf16[4,16,2944]{2,1,0:T(8,128)(2,1)S(1)}, bf16[4,16,2944]{2,1,0:T(8,128)(2,1)S(1)}, u32[]{:S(2)}, u32[]{:S(2)}) %collective-permute-start.13) | collective-permute-done | bytes 376864 | tf_op jit(solution)/shard_map/ppermute | solution.py:15
  92.3 3.8 %collective-permute-start.16 = (bf16[4,16,1536]{2,1,0:T(8,128)(2,1)S(1)}, bf16[4,16,1536]{2,1,0:T(8,128)(2,1)S(1)}, u32[]{:S(2)}, u32[]{:S(2)}) collective-permute-start(bf16[4,16,1536]{2,1,0:T(8,128)(2,1)S(1)} %slice.454), channel_id=1, source_target_pairs={{0,12},{4,0},{8,4},{12,8},{1,13},{5,1},{9,5},{13,9},{2,14},{6,2},{... | collective-permute-start | bytes 589832 | tf_op jit(solution)/shard_map/ppermute | solution.py:15
  96.2 1.5 %collective-permute-start.29 = (bf16[4,16,1536]{2,1,0:T(8,128)(2,1)S(1)}, bf16[4,16,1536]{2,1,0:T(8,128)(2,1)S(1)}, u32[]{:S(2)}, u32[]{:S(2)}) collective-permute-start(bf16[4,16,1536]{2,1,0:T(8,128)(2,1)S(1)} %slice.472), channel_id=1, source_target_pairs={{0,3},{1,0},{2,1},{3,2},{4,7},{5,4},{6,5},{7,6},{8,11},{9,8},{10,9... | collective-permute-start | bytes 589832 | tf_op jit(solution)/shard_map/ppermute | solution.py:15
  98.4 4.5 %collective-permute-done.15 = bf16[4,16,1408]{2,1,0:T(8,128)(2,1)S(1)} collective-permute-done((bf16[4,16,1408]{2,1,0:T(8,128)(2,1)S(1)}, bf16[4,16,1408]{2,1,0:T(8,128)(2,1)S(1)}, u32[]{:S(2)}, u32[]{:S(2)}) %collective-permute-start.15) | collective-permute-done | bytes 180256 | tf_op jit(solution)/shard_map/ppermute | solution.py:15
  109.2 1.8 %fusion.10 = f32[256,512]{1,0:T(8,128)S(1)} fusion(bf16[1920,512]{1,0:T(8,128)(2,1)} %param.10, bf16[256,3072]{1,0:T(8,128)(2,1)S(1)} %bitcast.200), kind=kOutput, calls=%fused_computation.44 | convolution fusion | flops 268435456 | bytes 2097152 | tf_op jit(solution)/shard_map/dot_general | solution.py:28
  113.7 1.8 %fusion.3 = bf16[256,64]{1,0:T(8,128)(2,1)} fusion(f32[256,64]{1,0:T(8,128)S(1)} %copy-done.33, bf16[256,2944]{1,0:T(8,128)(2,1)S(1)} %bitcast.192, bf16[64,1920]{1,0:T(8,128)(2,1)} %copy-done.9), kind=kOutput, calls=%fused_computation.26 | convolution fusion | flops 29392896 | bytes 737280 | tf_op jit(solution)/shard_map/dot_general | solution.py:28
  115.5 1.9 %fusion.4 = bf16[256,64]{1,0:T(8,128)(2,1)} fusion(f32[256,64]{1,0:T(8,128)S(1)} %copy-done.32, bf16[256,2944]{1,0:T(8,128)(2,1)S(1)} %bitcast.193, bf16[64,1920]{1,0:T(8,128)(2,1)} %copy-done.13), kind=kOutput, calls=%fused_computation.27 | convolution fusion | flops 29392896 | bytes 737280 | tf_op jit(solution)/shard_map/dot_general | solution.py:28
  119.6 1.7 %fusion.2 = bf16[256,512]{1,0:T(8,128)(2,1)S(1)} fusion(f32[256,512]{1,0:T(8,128)S(1)} %convolution_multiply_fusion, f32[256,512]{1,0:T(8,128)S(1)} %fusion.10, bf16[1920,512]{1,0:T(8,128)(2,1)} %param.10, bf16[256,2944]{1,0:T(8,128)(2,1)S(1)} %bitcast.196), kind=kOutput, calls=%fused_computation.21 | convolution fusion | flops 235274240 | bytes 2686976 | tf_op jit(solution)/shard_map/dot_general | solution.py:28
  125.8 2.6 %collective-permute-start.32 = (bf16[32,2048]{1,0:T(8,128)(2,1)S(1)}, bf16[32,2048]{1,0:T(8,128)(2,1)S(1)}, u32[]{:S(2)}, u32[]{:S(2)}) collective-permute-start(bf16[32,2048]{1,0:T(8,128)(2,1)S(1)} %get-tuple-element.30), channel_id=1, source_target_pairs={{0,96},{16,112},{32,0},{48,16},{64,32},{80,48},{96,64},{112,80},{1... | collective-permute-start | bytes 393224 | tf_op jit(solution)/shard_map/ppermute | solution.py:24
  128.4 5.3 %collective-permute-done.31 = bf16[32,2048]{1,0:T(8,128)(2,1)S(1)} collective-permute-done((bf16[32,2048]{1,0:T(8,128)(2,1)S(1)}, bf16[32,2048]{1,0:T(8,128)(2,1)S(1)}, u32[]{:S(2)}, u32[]{:S(2)}) %collective-permute-start.31) | collective-permute-done | bytes 131104 | tf_op jit(solution)/shard_map/ppermute | solution.py:24
  133.7 1.4 %collective-permute-done.32 = bf16[32,2048]{1,0:T(8,128)(2,1)S(1)} collective-permute-done((bf16[32,2048]{1,0:T(8,128)(2,1)S(1)}, bf16[32,2048]{1,0:T(8,128)(2,1)S(1)}, u32[]{:S(2)}, u32[]{:S(2)}) %collective-permute-start.32) | collective-permute-done | bytes 131104 | tf_op jit(solution)/shard_map/ppermute | solution.py:24
  (208 shorter events, 40.2 us)
Async XLA Ops:
  6.3 9.1 %collective-permute-start.1 = (bf16[64,1024]{1,0:T(8,128)(2,1)S(1)}, bf16[64,1024]{1,0:T(8,128)(2,1)S(1)}, u32[]{:S(2)}, u32[]{:S(2)}) collective-permute-start(bf16[64,1024]{1,0:T(8,128)(2,1)S(1)} %pad_maximum_fusion.5), channel_id=1, source_target_pairs={{0,96},{16,112},{32,0},{48,16},{64,32},{80,48},{96,64},{112,80},{1... | collective-permute-start | bytes 393224 | tf_op jit(solution)/shard_map/ppermute | solution.py:24
  9.2 8.0 %collective-permute-start.2 = (bf16[64,1024]{1,0:T(8,128)(2,1)S(1)}, bf16[64,1024]{1,0:T(8,128)(2,1)S(1)}, u32[]{:S(2)}, u32[]{:S(2)}) collective-permute-start(bf16[64,1024]{1,0:T(8,128)(2,1)S(1)} %pad_maximum_fusion.5), channel_id=1, source_target_pairs={{0,64},{16,80},{32,96},{48,112},{64,0},{80,16},{96,32},{112,48},{1... | collective-permute-start | bytes 393224 | tf_op jit(solution)/shard_map/ppermute | solution.py:24
  10.1 9.1 %collective-permute-start.3 = (bf16[64,1024]{1,0:T(8,128)(2,1)S(1)}, bf16[64,1024]{1,0:T(8,128)(2,1)S(1)}, u32[]{:S(2)}, u32[]{:S(2)}) collective-permute-start(bf16[64,1024]{1,0:T(8,128)(2,1)S(1)} %pad_maximum_fusion.5), channel_id=1, source_target_pairs={{0,32},{16,48},{32,64},{48,80},{64,96},{80,112},{96,0},{112,16},{1... | collective-permute-start | bytes 393224 | tf_op jit(solution)/shard_map/ppermute | solution.py:24
  30.2 19.4 %collective-permute-start.6 = (bf16[4,16,2944]{2,1,0:T(8,128)(2,1)S(1)}, bf16[4,16,2944]{2,1,0:T(8,128)(2,1)S(1)}, u32[]{:S(2)}, u32[]{:S(2)}) collective-permute-start(bf16[4,16,2944]{2,1,0:T(8,128)(2,1)S(1)} %bitcast.221), channel_id=1, source_target_pairs={{0,12},{4,0},{8,4},{12,8},{1,13},{5,1},{9,5},{13,9},{2,14},{6,2},{... | collective-permute-start | bytes 1130504 | tf_op jit(solution)/shard_map/ppermute | solution.py:15
  33.3 18.2 %collective-permute-start.5 = (bf16[4,16,2944]{2,1,0:T(8,128)(2,1)S(1)}, bf16[4,16,2944]{2,1,0:T(8,128)(2,1)S(1)}, u32[]{:S(2)}, u32[]{:S(2)}) collective-permute-start(bf16[4,16,2944]{2,1,0:T(8,128)(2,1)S(1)} %bitcast.220), channel_id=1, source_target_pairs={{0,8},{4,12},{8,0},{12,4},{1,9},{5,13},{9,1},{13,5},{2,10},{6,14},... | collective-permute-start | bytes 1130504 | tf_op jit(solution)/shard_map/ppermute | solution.py:15
  33.9 19.4 %collective-permute-start.4 = (bf16[4,16,2944]{2,1,0:T(8,128)(2,1)S(1)}, bf16[4,16,2944]{2,1,0:T(8,128)(2,1)S(1)}, u32[]{:S(2)}, u32[]{:S(2)}) collective-permute-start(bf16[4,16,2944]{2,1,0:T(8,128)(2,1)S(1)} %bitcast.219), channel_id=1, source_target_pairs={{0,4},{4,8},{8,12},{12,0},{1,5},{5,9},{9,13},{13,1},{2,6},{6,10},{... | collective-permute-start | bytes 1130504 | tf_op jit(solution)/shard_map/ppermute | solution.py:15
  35.1 22.5 %collective-permute-start.19 = (bf16[4,16,3072]{2,1,0:T(8,128)(2,1)S(1)}, bf16[4,16,3072]{2,1,0:T(8,128)(2,1)S(1)}, u32[]{:S(2)}, u32[]{:S(2)}) collective-permute-start(bf16[4,16,3072]{2,1,0:T(8,128)(2,1)S(1)} %get-tuple-element.11), channel_id=1, source_target_pairs={{0,3},{1,0},{2,1},{3,2},{4,7},{5,4},{6,5},{7,6},{8,11},{9,8},{10,9... | collective-permute-start | bytes 1179656 | tf_op jit(solution)/shard_map/ppermute | solution.py:15
  39.2 19.7 %collective-permute-start.18 = (bf16[4,16,3072]{2,1,0:T(8,128)(2,1)S(1)}, bf16[4,16,3072]{2,1,0:T(8,128)(2,1)S(1)}, u32[]{:S(2)}, u32[]{:S(2)}) collective-permute-start(bf16[4,16,3072]{2,1,0:T(8,128)(2,1)S(1)} %get-tuple-element.12), channel_id=1, source_target_pairs={{0,2},{1,3},{2,0},{3,1},{4,6},{5,7},{6,4},{7,5},{8,10},{9,11},{10,... | collective-permute-start | bytes 1179656 | tf_op jit(solution)/shard_map/ppermute | solution.py:15
  49.6 14.1 %collective-permute-start.17 = (bf16[4,16,3072]{2,1,0:T(8,128)(2,1)S(1)}, bf16[4,16,3072]{2,1,0:T(8,128)(2,1)S(1)}, u32[]{:S(2)}, u32[]{:S(2)}) collective-permute-start(bf16[4,16,3072]{2,1,0:T(8,128)(2,1)S(1)} %get-tuple-element.10), channel_id=1, source_target_pairs={{0,1},{1,2},{2,3},{3,0},{4,5},{5,6},{6,7},{7,4},{8,9},{9,10},{10,1... | collective-permute-start | bytes 1179656 | tf_op jit(solution)/shard_map/ppermute | solution.py:15
  53.5 14.6 %collective-permute-start.9 = (bf16[16,2944]{1,0:T(8,128)(2,1)S(1)}, bf16[16,2944]{1,0:T(8,128)(2,1)S(1)}, u32[]{:S(2)}, u32[]{:S(2)}) collective-permute-start(bf16[16,2944]{1,0:T(8,128)(2,1)S(1)} %get-tuple-element.27), channel_id=1, source_target_pairs={{0,3},{1,0},{2,1},{3,2},{4,7},{5,4},{6,5},{7,6},{8,11},{9,8},{10,9... | collective-permute-start | bytes 282632 | tf_op jit(solution)/shard_map/ppermute | solution.py:15
  57.6 11.4 %collective-permute-start.8 = (bf16[16,2944]{1,0:T(8,128)(2,1)S(1)}, bf16[16,2944]{1,0:T(8,128)(2,1)S(1)}, u32[]{:S(2)}, u32[]{:S(2)}) collective-permute-start(bf16[16,2944]{1,0:T(8,128)(2,1)S(1)} %get-tuple-element.28), channel_id=1, source_target_pairs={{0,2},{1,3},{2,0},{3,1},{4,6},{5,7},{6,4},{7,5},{8,10},{9,11},{10,... | collective-permute-start | bytes 282632 | tf_op jit(solution)/shard_map/ppermute | solution.py:15
  57.6 11.4 %collective-permute-start.7 = (bf16[16,2944]{1,0:T(8,128)(2,1)S(1)}, bf16[16,2944]{1,0:T(8,128)(2,1)S(1)}, u32[]{:S(2)}, u32[]{:S(2)}) collective-permute-start(bf16[16,2944]{1,0:T(8,128)(2,1)S(1)} %get-tuple-element.26), channel_id=1, source_target_pairs={{0,1},{1,2},{2,3},{3,0},{4,5},{5,6},{6,7},{7,4},{8,9},{9,10},{10,1... | collective-permute-start | bytes 282632 | tf_op jit(solution)/shard_map/ppermute | solution.py:15
  63.9 9.7 %collective-permute-start.22 = (bf16[16,3072]{1,0:T(8,128)(2,1)S(1)}, bf16[16,3072]{1,0:T(8,128)(2,1)S(1)}, u32[]{:S(2)}, u32[]{:S(2)}) collective-permute-start(bf16[16,3072]{1,0:T(8,128)(2,1)S(1)} %get-tuple-element.22), channel_id=1, source_target_pairs={{0,12},{4,0},{8,4},{12,8},{1,13},{5,1},{9,5},{13,9},{2,14},{6,2},{... | collective-permute-start | bytes 294920 | tf_op jit(solution)/shard_map/ppermute | solution.py:15
  68.1 7.8 %collective-permute-start.21 = (bf16[16,3072]{1,0:T(8,128)(2,1)S(1)}, bf16[16,3072]{1,0:T(8,128)(2,1)S(1)}, u32[]{:S(2)}, u32[]{:S(2)}) collective-permute-start(bf16[16,3072]{1,0:T(8,128)(2,1)S(1)} %get-tuple-element.23), channel_id=1, source_target_pairs={{0,8},{4,12},{8,0},{12,4},{1,9},{5,13},{9,1},{13,5},{2,10},{6,14},... | collective-permute-start | bytes 294920 | tf_op jit(solution)/shard_map/ppermute | solution.py:15
  68.1 7.8 %collective-permute-start.20 = (bf16[16,3072]{1,0:T(8,128)(2,1)S(1)}, bf16[16,3072]{1,0:T(8,128)(2,1)S(1)}, u32[]{:S(2)}, u32[]{:S(2)}) collective-permute-start(bf16[16,3072]{1,0:T(8,128)(2,1)S(1)} %get-tuple-element.21), channel_id=1, source_target_pairs={{0,4},{4,8},{8,12},{12,0},{1,5},{5,9},{9,13},{13,1},{2,6},{6,10},{... | collective-permute-start | bytes 294920 | tf_op jit(solution)/shard_map/ppermute | solution.py:15
  70.6 9.7 %collective-permute-start.12 = (bf16[16,2944]{1,0:T(8,128)(2,1)S(1)}, bf16[16,2944]{1,0:T(8,128)(2,1)S(1)}, u32[]{:S(2)}, u32[]{:S(2)}) collective-permute-start(bf16[16,2944]{1,0:T(8,128)(2,1)S(1)} %concatenate.67), channel_id=1, source_target_pairs={{0,1},{1,2},{2,3},{3,0},{4,5},{5,6},{6,7},{7,4},{8,9},{9,10},{10,1... | collective-permute-start | bytes 282632 | tf_op jit(solution)/shard_map/ppermute | solution.py:15
  70.7 11.1 %collective-permute-start.11 = (bf16[16,2944]{1,0:T(8,128)(2,1)S(1)}, bf16[16,2944]{1,0:T(8,128)(2,1)S(1)}, u32[]{:S(2)}, u32[]{:S(2)}) collective-permute-start(bf16[16,2944]{1,0:T(8,128)(2,1)S(1)} %concatenate.67), channel_id=1, source_target_pairs={{0,2},{1,3},{2,0},{3,1},{4,6},{5,7},{6,4},{7,5},{8,10},{9,11},{10,... | collective-permute-start | bytes 282632 | tf_op jit(solution)/shard_map/ppermute | solution.py:15
  73.6 8.2 %collective-permute-start.10 = (bf16[16,2944]{1,0:T(8,128)(2,1)S(1)}, bf16[16,2944]{1,0:T(8,128)(2,1)S(1)}, u32[]{:S(2)}, u32[]{:S(2)}) collective-permute-start(bf16[16,2944]{1,0:T(8,128)(2,1)S(1)} %concatenate.67), channel_id=1, source_target_pairs={{0,3},{1,0},{2,1},{3,2},{4,7},{5,4},{6,5},{7,6},{8,11},{9,8},{10,9... | collective-permute-start | bytes 282632 | tf_op jit(solution)/shard_map/ppermute | solution.py:15
  76.4 8.8 %collective-permute-start.25 = (bf16[16,3072]{1,0:T(8,128)(2,1)S(1)}, bf16[16,3072]{1,0:T(8,128)(2,1)S(1)}, u32[]{:S(2)}, u32[]{:S(2)}) collective-permute-start(bf16[16,3072]{1,0:T(8,128)(2,1)S(1)} %get-tuple-element.67), channel_id=1, source_target_pairs={{0,4},{4,8},{8,12},{12,0},{1,5},{5,9},{9,13},{13,1},{2,6},{6,10},{... | collective-permute-start | bytes 294920 | tf_op jit(solution)/shard_map/ppermute | solution.py:15
  79.0 6.2 %collective-permute-start.24 = (bf16[16,3072]{1,0:T(8,128)(2,1)S(1)}, bf16[16,3072]{1,0:T(8,128)(2,1)S(1)}, u32[]{:S(2)}, u32[]{:S(2)}) collective-permute-start(bf16[16,3072]{1,0:T(8,128)(2,1)S(1)} %get-tuple-element.67), channel_id=1, source_target_pairs={{0,8},{4,12},{8,0},{12,4},{1,9},{5,13},{9,1},{13,5},{2,10},{6,14},... | collective-permute-start | bytes 294920 | tf_op jit(solution)/shard_map/ppermute | solution.py:15
  80.3 5.0 %collective-permute-start.23 = (bf16[16,3072]{1,0:T(8,128)(2,1)S(1)}, bf16[16,3072]{1,0:T(8,128)(2,1)S(1)}, u32[]{:S(2)}, u32[]{:S(2)}) collective-permute-start(bf16[16,3072]{1,0:T(8,128)(2,1)S(1)} %get-tuple-element.67), channel_id=1, source_target_pairs={{0,12},{4,0},{8,4},{12,8},{1,13},{5,1},{9,5},{13,9},{2,14},{6,2},{... | collective-permute-start | bytes 294920 | tf_op jit(solution)/shard_map/ppermute | solution.py:15
  81.9 14.1 %collective-permute-start.14 = (bf16[4,16,2944]{2,1,0:T(8,128)(2,1)S(1)}, bf16[4,16,2944]{2,1,0:T(8,128)(2,1)S(1)}, u32[]{:S(2)}, u32[]{:S(2)}) collective-permute-start(bf16[4,16,2944]{2,1,0:T(8,128)(2,1)S(1)} %get-tuple-element.25), channel_id=1, source_target_pairs={{0,4},{4,8},{8,12},{12,0},{1,5},{5,9},{9,13},{13,1},{2,6},{6,10},{... | collective-permute-start | bytes 1130504 | tf_op jit(solution)/shard_map/ppermute | solution.py:15
  82.4 9.8 %collective-permute-start.13 = (bf16[4,16,2944]{2,1,0:T(8,128)(2,1)S(1)}, bf16[4,16,2944]{2,1,0:T(8,128)(2,1)S(1)}, u32[]{:S(2)}, u32[]{:S(2)}) collective-permute-start(bf16[4,16,2944]{2,1,0:T(8,128)(2,1)S(1)} %get-tuple-element.25), channel_id=1, source_target_pairs={{0,12},{4,0},{8,4},{12,8},{1,13},{5,1},{9,5},{13,9},{2,14},{6,2},{... | collective-permute-start | bytes 1130504 | tf_op jit(solution)/shard_map/ppermute | solution.py:15
  85.3 10.8 %collective-permute-start.26 = (bf16[4,16,3072]{2,1,0:T(8,128)(2,1)S(1)}, bf16[4,16,3072]{2,1,0:T(8,128)(2,1)S(1)}, u32[]{:S(2)}, u32[]{:S(2)}) collective-permute-start(bf16[4,16,3072]{2,1,0:T(8,128)(2,1)S(1)} %get-tuple-element.20), channel_id=1, source_target_pairs={{0,3},{1,0},{2,1},{3,2},{4,7},{5,4},{6,5},{7,6},{8,11},{9,8},{10,9... | collective-permute-start | bytes 1179656 | tf_op jit(solution)/shard_map/ppermute | solution.py:15
  86.5 11.2 %collective-permute-start.27 = (bf16[4,16,3072]{2,1,0:T(8,128)(2,1)S(1)}, bf16[4,16,3072]{2,1,0:T(8,128)(2,1)S(1)}, u32[]{:S(2)}, u32[]{:S(2)}) collective-permute-start(bf16[4,16,3072]{2,1,0:T(8,128)(2,1)S(1)} %get-tuple-element.20), channel_id=1, source_target_pairs={{0,1},{1,2},{2,3},{3,0},{4,5},{5,6},{6,7},{7,4},{8,9},{9,10},{10,1... | collective-permute-start | bytes 1179656 | tf_op jit(solution)/shard_map/ppermute | solution.py:15
  92.3 10.6 %collective-permute-start.16 = (bf16[4,16,1536]{2,1,0:T(8,128)(2,1)S(1)}, bf16[4,16,1536]{2,1,0:T(8,128)(2,1)S(1)}, u32[]{:S(2)}, u32[]{:S(2)}) collective-permute-start(bf16[4,16,1536]{2,1,0:T(8,128)(2,1)S(1)} %slice.454), channel_id=1, source_target_pairs={{0,12},{4,0},{8,4},{12,8},{1,13},{5,1},{9,5},{13,9},{2,14},{6,2},{... | collective-permute-start | bytes 589832 | tf_op jit(solution)/shard_map/ppermute | solution.py:15
  96.1 6.8 %collective-permute-start.15 = (bf16[4,16,1408]{2,1,0:T(8,128)(2,1)S(1)}, bf16[4,16,1408]{2,1,0:T(8,128)(2,1)S(1)}, u32[]{:S(2)}, u32[]{:S(2)}) collective-permute-start(bf16[4,16,1408]{2,1,0:T(8,128)(2,1)S(1)} %slice.453), channel_id=1, source_target_pairs={{0,4},{4,8},{8,12},{12,0},{1,5},{5,9},{9,13},{13,1},{2,6},{6,10},{... | collective-permute-start | bytes 540680 | tf_op jit(solution)/shard_map/ppermute | solution.py:15
  96.2 9.8 %collective-permute-start.29 = (bf16[4,16,1536]{2,1,0:T(8,128)(2,1)S(1)}, bf16[4,16,1536]{2,1,0:T(8,128)(2,1)S(1)}, u32[]{:S(2)}, u32[]{:S(2)}) collective-permute-start(bf16[4,16,1536]{2,1,0:T(8,128)(2,1)S(1)} %slice.472), channel_id=1, source_target_pairs={{0,3},{1,0},{2,1},{3,2},{4,7},{5,4},{6,5},{7,6},{8,11},{9,8},{10,9... | collective-permute-start | bytes 589832 | tf_op jit(solution)/shard_map/ppermute | solution.py:15
  97.7 8.2 %collective-permute-start.28 = (bf16[4,16,1536]{2,1,0:T(8,128)(2,1)S(1)}, bf16[4,16,1536]{2,1,0:T(8,128)(2,1)S(1)}, u32[]{:S(2)}, u32[]{:S(2)}) collective-permute-start(bf16[4,16,1536]{2,1,0:T(8,128)(2,1)S(1)} %slice.471), channel_id=1, source_target_pairs={{0,1},{1,2},{2,3},{3,0},{4,5},{5,6},{6,7},{7,4},{8,9},{9,10},{10,1... | collective-permute-start | bytes 589832 | tf_op jit(solution)/shard_map/ppermute | solution.py:15
  124.0 9.6 %collective-permute-start.31 = (bf16[32,2048]{1,0:T(8,128)(2,1)S(1)}, bf16[32,2048]{1,0:T(8,128)(2,1)S(1)}, u32[]{:S(2)}, u32[]{:S(2)}) collective-permute-start(bf16[32,2048]{1,0:T(8,128)(2,1)S(1)} %get-tuple-element.29), channel_id=1, source_target_pairs={{0,32},{16,48},{32,64},{48,80},{64,96},{80,112},{96,0},{112,16},{1... | collective-permute-start | bytes 393224 | tf_op jit(solution)/shard_map/ppermute | solution.py:24
  124.9 10.2 %collective-permute-start.33 = (bf16[32,2048]{1,0:T(8,128)(2,1)S(1)}, bf16[32,2048]{1,0:T(8,128)(2,1)S(1)}, u32[]{:S(2)}, u32[]{:S(2)}) collective-permute-start(bf16[32,2048]{1,0:T(8,128)(2,1)S(1)} %get-tuple-element.31), channel_id=1, source_target_pairs={{0,64},{16,80},{32,96},{48,112},{64,0},{80,16},{96,32},{112,48},{1... | collective-permute-start | bytes 393224 | tf_op jit(solution)/shard_map/ppermute | solution.py:24
  125.8 9.3 %collective-permute-start.32 = (bf16[32,2048]{1,0:T(8,128)(2,1)S(1)}, bf16[32,2048]{1,0:T(8,128)(2,1)S(1)}, u32[]{:S(2)}, u32[]{:S(2)}) collective-permute-start(bf16[32,2048]{1,0:T(8,128)(2,1)S(1)} %get-tuple-element.30), channel_id=1, source_target_pairs={{0,96},{16,112},{32,0},{48,16},{64,32},{80,48},{96,64},{112,80},{1... | collective-permute-start | bytes 393224 | tf_op jit(solution)/shard_map/ppermute | solution.py:24
  (37 other events, 381.6 us)
